TPU v7x, 32 devices: a whole 2x2x4 slice. The times are simulated.
32 devices in a mesh: row: 8 (over z, x), col: 4 (over y, core).
Axes of the slice: x: 2, y: 2, z: 4, core: 2. Of those that a mesh axis runs over, the one named last changes fastest.
Arguments:
- pair: bfloat16 [64, 64, 128], P('row', 'col'), may hold values from -6 to 6
- norm_in: float32 [128], replicated, may hold values from 0.1 to 1.9
- shift_in: float32 [128], replicated, may hold values from -3 to 3
- in_weight: bfloat16 [128, 640], replicated, may hold values from -0.5 to 0.5
- norm_out: float32 [128], replicated, may hold values from 0.1 to 1.9
- shift_out: float32 [128], replicated, may hold values from -3 to 3
- out_weight: bfloat16 [128, 128], replicated, may hold values from -0.5 to 0.5
Outputs:
- update: bfloat16 [64, 64, 128], P('row', 'col')
All inputs are finite; a program needn't handle non-finite values.
Results may differ from a plain program's by a relative error of at most 0.0054.
Values may be sent and summed in bfloat16 or wider, within the bound.
A program may use at most 64 MiB of HBM per device.

v0:
```python
import jax
import jax.numpy as jnp
from jax import lax
from jax.sharding import PartitionSpec as P

EPSILON = 1e-05


def layer_norm(values, gain, shift):
    values = values.astype(jnp.float32)
    center = jnp.mean(values, axis=-1, keepdims=True)
    spread = jnp.mean(jnp.square(values - center), axis=-1, keepdims=True)
    return (values - center) * lax.rsqrt(spread + EPSILON) * gain + shift


def local(pair, norm_in, shift_in, in_weight, norm_out, shift_out, out_weight):
    row_count, col_count, channels = pair.shape
    hidden = out_weight.shape[0]
    normed = layer_norm(pair, norm_in, shift_in).astype(jnp.bfloat16)
    projected = jnp.dot(normed.reshape(-1, channels), in_weight, preferred_element_type=jnp.float32)
    left = (jax.nn.sigmoid(projected[:, :hidden]) * projected[:, hidden : 2 * hidden]).astype(
        jnp.bfloat16
    )
    right = (
        jax.nn.sigmoid(projected[:, 2 * hidden : 3 * hidden])
        * projected[:, 3 * hidden : 4 * hidden]
    ).astype(jnp.bfloat16)
    gate = jax.nn.sigmoid(projected[:, 4 * hidden :]).reshape(row_count, col_count, channels)
    left = left.reshape(row_count, col_count, hidden)
    right = right.reshape(row_count, col_count, hidden)
    row_devices = lax.axis_size("row")
    col_devices = lax.axis_size("col")
    unit = row_count // col_devices
    groups = row_devices // col_devices
    sectioned = left.reshape(row_count, groups, col_devices, unit, hidden).transpose(0, 2, 1, 3, 4)
    sorted_parts = lax.all_to_all(sectioned, "col", split_axis=1, concat_axis=1, tiled=True)
    sorted_parts = sorted_parts.reshape(row_count, row_devices, unit * hidden)
    own_parts = lax.all_to_all(sorted_parts, "row", split_axis=1, concat_axis=0, tiled=True)
    own_parts = own_parts.reshape(row_count * row_devices, unit, hidden)
    right_full = lax.all_gather(right, "row", axis=0, tiled=True)
    mixed = jnp.einsum(
        "kih,kjh->ijh",
        lax.all_gather(own_parts, "col", axis=1, tiled=True),
        right_full,
        preferred_element_type=jnp.float32,
    )
    mixed_normed = layer_norm(mixed, norm_out, shift_out).astype(jnp.bfloat16)
    outward = jnp.dot(
        mixed_normed.reshape(-1, hidden), out_weight, preferred_element_type=jnp.float32
    )
    return (gate * outward.reshape(row_count, col_count, channels)).astype(jnp.bfloat16)


def solution(mesh):
    in_specs = (P("row", "col", None), P(), P(), P(), P(), P(), P())
    out_specs = P("row", "col", None)
    return jax.shard_map(local, mesh=mesh, in_specs=in_specs, out_specs=out_specs, check_vma=False)
```

profile of v0, /device:TPU:0, one launch (start us, length us, event | category | flops | bytes accessed | tf_op | source)
XLA Modules:
  0.0 71.7 jit_solution(3137486336146539258)
XLA Ops:
  0.0 0.0 copy-start
  0.0 0.9 %convert_reduce_fusion = f32[8,16]{1,0:T(8,128)S(1)} fusion(bf16[8,16,128]{2,1,0:T(8,128)(2,1)} %param.7), kind=kLoop, calls=%fused_computation.3 | loop fusion | flops 32640 | bytes 33280 | tf_op jit(solution)/shard_map/reduce_sum | solution.py:11
  0.9 0.9 %fusion.3 = f32[8,16]{1,0:T(8,128)S(1)} fusion(bf16[8,16,128]{2,1,0:T(8,128)(2,1)} %param.7, f32[8,16]{1,0:T(8,128)S(1)} %broadcast_multiply_fusion.1), kind=kLoop, calls=%fused_computation.6 | loop fusion | flops 65408 | bytes 33792 | tf_op jit(solution)/shard_map/reduce_sum | solution.py:12
  1.8 0.9 %fusion.6 = bf16[8,16,128]{2,1,0:T(8,128)(2,1)S(1)} fusion(bf16[8,16,128]{2,1,0:T(8,128)(2,1)} %param.7, f32[128]{0:T(128)} %param.9, f32[128]{0:T(128)} %param.8, f32[8,16]{1,0:T(8,128)S(1)} %add_rsqrt_fusion.1, f32[8,16]{1,0:T(8,128)S(1)} %broadcast_multiply_fusion.1), kind=kLoop, calls=%fused_computation.9 | loop fusion | flops 98304 | bytes 67584 | tf_op jit(solution)/shard_map/convert_element_type | solution.py:19
  2.7 0.0 copy-done
  2.7 0.2 fusion.23
  2.9 0.1 fusion.7
  3.0 0.6 copy.32
  3.6 4.3 %all-to-all-start = ((bf16[8,4,2,2,128]{4,3,2,0,1:T(2,128)(2,1)}), bf16[8,4,2,2,128]{4,3,2,0,1:T(2,128)(2,1)S(1)}, u32[]{:S(2)}, u32[]{:S(2)}) async-start(bf16[8,4,2,2,128]{4,3,2,0,1:T(2,128)(2,1)} %bitcast.30), calls=%async_computation | async-start | bytes 65536 | tf_op jit(solution)/shard_map/all_to_all | solution.py:36
  7.9 0.2 copy.22
  8.1 3.8 %all-to-all-done = bf16[8,4,2,2,128]{4,3,2,0,1:T(2,128)(2,1)S(1)} async-done(((bf16[8,4,2,2,128]{4,3,2,0,1:T(2,128)(2,1)}), bf16[8,4,2,2,128]{4,3,2,0,1:T(2,128)(2,1)S(1)}, u32[]{:S(2)}, u32[]{:S(2)}) %all-to-all-start) | async-done | bytes 32800 | tf_op jit(solution)/shard_map/all_to_all | solution.py:36
  11.9 0.6 reshape.54
  12.5 6.3 %all-to-all-start.1 = ((bf16[8,8,256]{2,0,1:T(8,128)(2,1)}), bf16[8,8,256]{2,0,1:T(8,128)(2,1)S(1)}, u32[]{:S(2)}, u32[]{:S(2)}) async-start(bf16[8,8,256]{2,0,1:T(8,128)(2,1)} %reshape.54), calls=%async_computation.1 | async-start | bytes 65536 | tf_op jit(solution)/shard_map/all_to_all | solution.py:38
  18.8 45.2 %all_gather.6 = bf16[64,16,128]{1,0,2:T(8,128)(2,1)S(1)} all-gather(bf16[8,16,128]{1,0,2:T(8,128)(2,1)S(1)} %copy.22), channel_id=1, replica_groups=mesh['row'=8,'col'=4] {'row'}, dimensions={0}, use_global_device_ids=true | all-gather | bytes 294912 | tf_op jit(solution)/shard_map/all_gather | solution.py:40
  64.0 0.0 all-to-all-done.1
  64.0 0.0 copy-start.1
  64.1 0.0 copy-start.2
  64.1 0.0 copy-start.3
  64.1 5.4 %all_gather.7 = bf16[64,8,128]{2,0,1:T(8,128)(2,1)S(1)} all-gather(bf16[64,2,128]{2,0,1:T(8,128)(2,1)S(1)} %copy.26), channel_id=1, replica_groups=mesh['row'=8,'col'=4] {'col'}, dimensions={1}, use_global_device_ids=true | all-gather | bytes 163840 | tf_op jit(solution)/shard_map/all_gather | solution.py:43
  69.5 0.2 copy.27
  69.7 0.7 fusion.24
  70.3 0.2 copy.28
  70.5 0.1 bitcast_reduce_fusion
  70.7 0.2 multiply_reduce_fusion
  70.8 0.0 copy-done.1
  70.9 0.0 copy-done.2
  70.9 0.0 copy-done.3
  70.9 0.8 %fusion = bf16[8,16,128]{2,1,0:T(8,128)(2,1)} fusion(f32[8,16,128]{2,1,0:T(8,128)S(1)} %bitcast.31, f32[128,16,8]{0,1,2:T(8,128)S(1)} %copy.28, bf16[128,128]{1,0:T(8,128)(2,1)S(1)} %copy-done.1, f32[128]{0:T(128)S(1)} %copy-done.2, f32[128]{0:T(128)S(1)} %copy-done.3, f32[8,16]{1,0:T(8,128)S(1)} %add_rsqrt_fusion, f32[8,16]{1,0:T(8,128)S(1)} %broadcast_multiply_fusion), kind=kOutput, calls=%fused_computation.1 | convolution fusion | flops 4308992 | bytes 198656 | tf_op jit(solution)/shard_map/dot_general | solution.py:48
  (7 shorter events, 0.1 us)
Async XLA Ops:
  0.0 2.7 %copy-start = (bf16[128,640]{1,0:T(8,128)(2,1)S(1)}, bf16[128,640]{1,0:T(8,128)(2,1)}, u32[]{:S(2)}) copy-start(bf16[128,640]{1,0:T(8,128)(2,1)} %param.10) | copy-start | bytes 491524
  3.6 8.2 %all-to-all-start = ((bf16[8,4,2,2,128]{4,3,2,0,1:T(2,128)(2,1)}), bf16[8,4,2,2,128]{4,3,2,0,1:T(2,128)(2,1)S(1)}, u32[]{:S(2)}, u32[]{:S(2)}) async-start(bf16[8,4,2,2,128]{4,3,2,0,1:T(2,128)(2,1)} %bitcast.30), calls=%async_computation | async-start | bytes 65536 | tf_op jit(solution)/shard_map/all_to_all | solution.py:36
  12.5 51.5 %all-to-all-start.1 = ((bf16[8,8,256]{2,0,1:T(8,128)(2,1)}), bf16[8,8,256]{2,0,1:T(8,128)(2,1)S(1)}, u32[]{:S(2)}, u32[]{:S(2)}) async-start(bf16[8,8,256]{2,0,1:T(8,128)(2,1)} %reshape.54), calls=%async_computation.1 | async-start | bytes 65536 | tf_op jit(solution)/shard_map/all_to_all | solution.py:38
  64.0 6.8 %copy-start.1 = (bf16[128,128]{1,0:T(8,128)(2,1)S(1)}, bf16[128,128]{1,0:T(8,128)(2,1)}, u32[]{:S(2)}) copy-start(bf16[128,128]{1,0:T(8,128)(2,1)} %param.13) | copy-start | bytes 98308
  64.1 6.8 %copy-start.2 = (f32[128]{0:T(128)S(1)}, f32[128]{0:T(128)}, u32[]{:S(2)}) copy-start(f32[128]{0:T(128)} %param.12) | copy-start | bytes 1540
  64.1 6.8 %copy-start.3 = (f32[128]{0:T(128)S(1)}, f32[128]{0:T(128)}, u32[]{:S(2)}) copy-start(f32[128]{0:T(128)} %param.11) | copy-start | bytes 1540
where the time goes:
time: 72.2 us; the launch traced here: 71.7 us
  blocking collectives  50.7 us (70%)
  starting transfers between devices  10.5 us (15%)
  waiting for transfers between devices  3.76 us (5%)
  other arithmetic  3.04 us (4%)
  local copies, waits for them, and re-layouts  1.92 us (3%)
  matrix products  1.67 us (2%)
    all_gather x1, blocking collectives, local(): right_full = lax.all_gather(right, 'row', axis=0, tiled=True)  45.2 us
    all_to_all x1, starting transfers between devices, local(): lax.all_to_all(sorted_parts, 'row', split_axis=1, concat_axis=0, tiled=True)  6.25 us
    all_gather x1, blocking collectives, local(): lax.all_gather(own_parts, 'col', axis=1, tiled=True)  5.42 us
    all_to_all x1, starting transfers between devices, local(): lax.all_to_all(sectioned, 'col', split_axis=1, concat_axis=1, tiled=True)  4.26 us
    all_to_all x1, waiting for transfers between devices, local(): lax.all_to_all(sectioned, 'col', split_axis=1, concat_axis=1, tiled=True)  3.76 us
  transfers between devices with their start and end apart: 2, of which 1 were waited for; matrix products, arithmetic and copies ran while one was open for 0% of the time, Pallas kernels for 0%

commit v1 on v0

--- a/solution.py
+++ b/solution.py
@@ -4,6 +4,29 @@
 from jax.sharding import PartitionSpec as P
 
 EPSILON = 1e-05
+
+
+def point_tails(matrix, base_x):
+    mesh_ax = "col"
+    tile_out = lax.axis_size(mesh_ax)
+    known = lax.axis_index(mesh_ax)
+    p_next, heard, current_block = (tile_out, known, matrix.shape[1])
+    copies = []
+    d = 0
+    while d < p_next:
+        local_out = (
+            lax.ppermute(
+                matrix, axis_name=mesh_ax, perm=[(nth, (nth + 1) % p_next) for nth in range(p_next)]
+            )
+            if d + 1 < p_next
+            else matrix
+        )
+        copies.append(base_x(matrix, (heard - d) % p_next * current_block))
+        matrix = local_out
+        d += 1
+    moved = jnp.concatenate(copies[::-1], axis=0)
+    plain = jnp.roll(moved, (heard + 1) * copies[0].shape[0], axis=0)
+    return plain
 
 
 def layer_norm(values, gain, shift):
@@ -38,11 +61,11 @@
     own_parts = lax.all_to_all(sorted_parts, "row", split_axis=1, concat_axis=0, tiled=True)
     own_parts = own_parts.reshape(row_count * row_devices, unit, hidden)
     right_full = lax.all_gather(right, "row", axis=0, tiled=True)
-    mixed = jnp.einsum(
-        "kih,kjh->ijh",
-        lax.all_gather(own_parts, "col", axis=1, tiled=True),
-        right_full,
-        preferred_element_type=jnp.float32,
+    mixed = point_tails(
+        own_parts,
+        lambda own_block, offset: jnp.einsum(
+            "kih,kjh->ijh", own_block, right_full, preferred_element_type=jnp.float32
+        ),
     )
     mixed_normed = layer_norm(mixed, norm_out, shift_out).astype(jnp.bfloat16)
     outward = jnp.dot(

time: 72.2 us -> 77.7 us (1.076)
  waiting for transfers between devices: 3.76 us -> 12.7 us
  blocking collectives: 50.7 us -> 45.2 us
  matrix products: 1.67 us -> 3.62 us
    ppermute x0 -> x3, waiting for transfers between devices: none -> 8.91 us  [point_tails(): lax.ppermute(matrix, axis_name=mesh_ax, perm=[(nth, (nth + 1) % p_next) f...]
    all_gather x1 -> x0, blocking collectives: 5.42 us -> none  [local(): lax.all_gather(own_parts, 'col', axis=1, tiled=True)]
    dot_general x1 -> x4, matrix products: 0.65 us -> 2.6 us  [local(): jnp.einsum('kih,kjh->ijh', own_block, right_full, preferred_element_type=...]
  transfers between devices with their start and end apart: 2 -> 5, of which waited for: 1 -> 4; matrix products, arithmetic and copies ran while one was open for 0% -> 3% of each run, Pallas kernels for 0% -> 0%
where the time goes in v1:
time: 77.7 us; the launch traced here: 77.3 us
  blocking collectives  45.2 us (58%)
  waiting for transfers between devices  12.7 us (16%)
  starting transfers between devices  10.6 us (14%)
  matrix products  3.62 us (5%)
  other arithmetic  3.02 us (4%)
  local copies, waits for them, and re-layouts  1.93 us (2%)
    all_gather x1, blocking collectives, local(): right_full = lax.all_gather(right, 'row', axis=0, tiled=True)  45.2 us
    ppermute x3, waiting for transfers between devices, point_tails(): lax.ppermute(matrix, axis_name=mesh_ax, perm=[(nth, (nth + 1) % p_next) f...  8.91 us
    all_to_all x1, starting transfers between devices, local(): lax.all_to_all(sorted_parts, 'row', split_axis=1, concat_axis=0, tiled=True)  6.25 us
    all_to_all x1, starting transfers between devices, local(): lax.all_to_all(sectioned, 'col', split_axis=1, concat_axis=1, tiled=True)  4.26 us
    all_to_all x1, waiting for transfers between devices, local(): lax.all_to_all(sectioned, 'col', split_axis=1, concat_axis=1, tiled=True)  3.76 us
    dot_general x4, matrix products, local(): jnp.einsum('kih,kjh->ijh', own_block, right_full, preferred_element_type=...  2.6 us
  transfers between devices with their start and end apart: 5, of which 4 were waited for; matrix products, arithmetic and copies ran while one was open for 3% of the time, Pallas kernels for 0%

profile of v1, /device:TPU:0, one launch (start us, length us, event | category | flops | bytes accessed | tf_op | source)
XLA Modules:
  0.0 77.3 jit_solution(12437827089898417168)
XLA Ops:
  0.0 0.0 copy-start
  0.0 0.9 %convert_reduce_fusion = f32[8,16]{1,0:T(8,128)S(1)} fusion(bf16[8,16,128]{2,1,0:T(8,128)(2,1)} %param.7), kind=kLoop, calls=%fused_computation.7 | loop fusion | flops 32640 | bytes 33280 | tf_op jit(solution)/shard_map/reduce_sum | solution.py:34
  0.9 0.9 %fusion.3 = f32[8,16]{1,0:T(8,128)S(1)} fusion(bf16[8,16,128]{2,1,0:T(8,128)(2,1)} %param.7, f32[8,16]{1,0:T(8,128)S(1)} %broadcast_multiply_fusion.1), kind=kLoop, calls=%fused_computation.10 | loop fusion | flops 65408 | bytes 33792 | tf_op jit(solution)/shard_map/reduce_sum | solution.py:35
  1.8 0.9 %fusion.6 = bf16[8,16,128]{2,1,0:T(8,128)(2,1)S(1)} fusion(bf16[8,16,128]{2,1,0:T(8,128)(2,1)} %param.7, f32[128]{0:T(128)} %param.9, f32[128]{0:T(128)} %param.8, f32[8,16]{1,0:T(8,128)S(1)} %add_rsqrt_fusion.1, f32[8,16]{1,0:T(8,128)S(1)} %broadcast_multiply_fusion.1), kind=kLoop, calls=%fused_computation.13 | loop fusion | flops 98304 | bytes 67584 | tf_op jit(solution)/shard_map/convert_element_type | solution.py:42
  2.7 0.0 copy-done
  2.7 0.2 fusion.24
  2.9 0.1 fusion.7
  3.0 0.6 copy.33
  3.6 4.3 %all-to-all-start = ((bf16[8,4,2,2,128]{4,3,2,0,1:T(2,128)(2,1)}), bf16[8,4,2,2,128]{4,3,2,0,1:T(2,128)(2,1)S(1)}, u32[]{:S(2)}, u32[]{:S(2)}) async-start(bf16[8,4,2,2,128]{4,3,2,0,1:T(2,128)(2,1)} %bitcast.36), calls=%async_computation | async-start | bytes 65536 | tf_op jit(solution)/shard_map/all_to_all | solution.py:59
  7.9 0.2 copy.16
  8.1 3.8 %all-to-all-done = bf16[8,4,2,2,128]{4,3,2,0,1:T(2,128)(2,1)S(1)} async-done(((bf16[8,4,2,2,128]{4,3,2,0,1:T(2,128)(2,1)}), bf16[8,4,2,2,128]{4,3,2,0,1:T(2,128)(2,1)S(1)}, u32[]{:S(2)}, u32[]{:S(2)}) %all-to-all-start) | async-done | bytes 32800 | tf_op jit(solution)/shard_map/all_to_all | solution.py:59
  11.9 0.6 reshape.54
  12.5 6.3 %all-to-all-start.1 = ((bf16[8,8,256]{2,0,1:T(8,128)(2,1)}), bf16[8,8,256]{2,0,1:T(8,128)(2,1)S(1)}, u32[]{:S(2)}, u32[]{:S(2)}) async-start(bf16[8,8,256]{2,0,1:T(8,128)(2,1)} %reshape.54), calls=%async_computation.1 | async-start | bytes 65536 | tf_op jit(solution)/shard_map/all_to_all | solution.py:61
  18.8 45.2 %all_gather.3 = bf16[64,16,128]{1,0,2:T(8,128)(2,1)S(1)} all-gather(bf16[8,16,128]{1,0,2:T(8,128)(2,1)S(1)} %copy.16), channel_id=1, replica_groups=mesh['row'=8,'col'=4] {'row'}, dimensions={0}, use_global_device_ids=true | all-gather | bytes 294912 | tf_op jit(solution)/shard_map/all_gather | solution.py:63
  64.0 0.0 all-to-all-done.1
  64.0 0.1 copy.20
  64.2 0.1 collective-permute-start
  64.2 0.7 convolution_bitcast_fusion
  64.9 0.1 copy.25
  64.9 3.0 %collective-permute-done = bf16[64,2,128]{0,1,2:T(2,128)(2,1)S(1)} collective-permute-done((bf16[64,2,128]{0,1,2:T(2,128)(2,1)S(1)}, bf16[64,2,128]{0,1,2:T(2,128)(2,1)S(1)}, u32[]{:S(2)}, u32[]{:S(2)}) %collective-permute-start) | collective-permute-done | bytes 32800 | tf_op jit(solution)/shard_map/ppermute | solution.py:18
  67.9 0.0 collective-permute-start.1
  67.9 0.7 convolution_bitcast_fusion.1
  68.6 0.1 copy.24
  68.6 0.0 copy-start.1
  68.6 0.0 copy-start.2
  68.6 0.0 copy-start.3
  68.6 3.0 %collective-permute-done.1 = bf16[64,2,128]{0,1,2:T(2,128)(2,1)S(1)} collective-permute-done((bf16[64,2,128]{0,1,2:T(2,128)(2,1)S(1)}, bf16[64,2,128]{0,1,2:T(2,128)(2,1)S(1)}, u32[]{:S(2)}, u32[]{:S(2)}) %collective-permute-start.1) | collective-permute-done | bytes 32800 | tf_op jit(solution)/shard_map/ppermute | solution.py:18
  71.6 0.0 collective-permute-start.2
  71.6 0.7 convolution_bitcast_fusion.2
  72.3 0.1 copy.23
  72.3 3.0 %collective-permute-done.2 = bf16[64,2,128]{0,1,2:T(2,128)(2,1)S(1)} collective-permute-done((bf16[64,2,128]{0,1,2:T(2,128)(2,1)S(1)}, bf16[64,2,128]{0,1,2:T(2,128)(2,1)S(1)}, u32[]{:S(2)}, u32[]{:S(2)}) %collective-permute-start.2) | collective-permute-done | bytes 32800 | tf_op jit(solution)/shard_map/ppermute | solution.py:18
  75.3 0.6 convolution_bitcast_fusion.3
  75.9 0.1 copy.22
  76.1 0.1 dynamic-slice_reduce_fusion
  76.2 0.2 multiply_reduce_fusion
  76.4 0.0 copy-done.1
  76.4 0.0 copy-done.2
  76.4 0.0 copy-done.3
  76.4 0.8 %fusion = bf16[8,16,128]{2,1,0:T(8,128)(2,1)} fusion(f32[8,16,128]{2,1,0:T(8,128)S(1)} %bitcast.37, f32[16,16,128]{2,1,0:T(8,128)S(1)} %constant_dynamic-update-slice_fusion, s32[]{:T(128)S(6)} %select_n.14, bf16[128,128]{1,0:T(8,128)(2,1)S(1)} %copy-done.1, f32[128]{0:T(128)S(1)} %copy-done.2, f32[128]{0:T(128)S(1)} %copy-done.3, ...), kind=kOutput, calls=%fused_computation.5 | convolution fusion | flops 4308992 | bytes 205828 | tf_op jit(solution)/shard_map/dot_general | solution.py:71
  (14 shorter events, 0.1 us)
Async XLA Ops:
  0.0 2.7 %copy-start = (bf16[128,640]{1,0:T(8,128)(2,1)S(1)}, bf16[128,640]{1,0:T(8,128)(2,1)}, u32[]{:S(2)}) copy-start(bf16[128,640]{1,0:T(8,128)(2,1)} %param.10) | copy-start | bytes 491524
  3.6 8.2 %all-to-all-start = ((bf16[8,4,2,2,128]{4,3,2,0,1:T(2,128)(2,1)}), bf16[8,4,2,2,128]{4,3,2,0,1:T(2,128)(2,1)S(1)}, u32[]{:S(2)}, u32[]{:S(2)}) async-start(bf16[8,4,2,2,128]{4,3,2,0,1:T(2,128)(2,1)} %bitcast.36), calls=%async_computation | async-start | bytes 65536 | tf_op jit(solution)/shard_map/all_to_all | solution.py:59
  12.5 51.5 %all-to-all-start.1 = ((bf16[8,8,256]{2,0,1:T(8,128)(2,1)}), bf16[8,8,256]{2,0,1:T(8,128)(2,1)S(1)}, u32[]{:S(2)}, u32[]{:S(2)}) async-start(bf16[8,8,256]{2,0,1:T(8,128)(2,1)} %reshape.54), calls=%async_computation.1 | async-start | bytes 65536 | tf_op jit(solution)/shard_map/all_to_all | solution.py:61
  64.2 3.7 %collective-permute-start = (bf16[64,2,128]{0,1,2:T(2,128)(2,1)S(1)}, bf16[64,2,128]{0,1,2:T(2,128)(2,1)S(1)}, u32[]{:S(2)}, u32[]{:S(2)}) collective-permute-start(bf16[64,2,128]{0,1,2:T(2,128)(2,1)S(1)} %copy.20), channel_id=1, source_target_pairs={{0,1},{1,2},{2,3},{3,0},{4,5},{5,6},{6,7},{7,4},{8,9},{9,10},{10,1... | collective-permute-start | bytes 98312 | tf_op jit(solution)/shard_map/ppermute | solution.py:18
  67.9 3.7 %collective-permute-start.1 = (bf16[64,2,128]{0,1,2:T(2,128)(2,1)S(1)}, bf16[64,2,128]{0,1,2:T(2,128)(2,1)S(1)}, u32[]{:S(2)}, u32[]{:S(2)}) collective-permute-start(bf16[64,2,128]{0,1,2:T(2,128)(2,1)S(1)} %collective-permute-done), channel_id=1, source_target_pairs={{0,1},{1,2},{2,3},{3,0},{4,5},{5,6},{6,7},{7,4},{8,9},{9,10},{10,1... | collective-permute-start | bytes 98312 | tf_op jit(solution)/shard_map/ppermute | solution.py:18
  68.6 7.8 %copy-start.1 = (bf16[128,128]{1,0:T(8,128)(2,1)S(1)}, bf16[128,128]{1,0:T(8,128)(2,1)}, u32[]{:S(2)}) copy-start(bf16[128,128]{1,0:T(8,128)(2,1)} %param.13) | copy-start | bytes 98308
  68.6 7.8 %copy-start.2 = (f32[128]{0:T(128)S(1)}, f32[128]{0:T(128)}, u32[]{:S(2)}) copy-start(f32[128]{0:T(128)} %param.12) | copy-start | bytes 1540
  68.6 7.8 %copy-start.3 = (f32[128]{0:T(128)S(1)}, f32[128]{0:T(128)}, u32[]{:S(2)}) copy-start(f32[128]{0:T(128)} %param.11) | copy-start | bytes 1540
  71.6 3.7 %collective-permute-start.2 = (bf16[64,2,128]{0,1,2:T(2,128)(2,1)S(1)}, bf16[64,2,128]{0,1,2:T(2,128)(2,1)S(1)}, u32[]{:S(2)}, u32[]{:S(2)}) collective-permute-start(bf16[64,2,128]{0,1,2:T(2,128)(2,1)S(1)} %collective-permute-done.1), channel_id=1, source_target_pairs={{0,1},{1,2},{2,3},{3,0},{4,5},{5,6},{6,7},{7,4},{8,9},{9,10},{10,1... | collective-permute-start | bytes 98312 | tf_op jit(solution)/shard_map/ppermute | solution.py:18
